TPU v7x, 32 devices: a whole 2x2x4 slice. The times are simulated.
32 devices in a mesh: ctx: 2 (over x), tp: 4 (over y, core), dp: 4 (over z).
Axes of the slice: x: 2, y: 2, z: 4, core: 2. Of those that a mesh axis runs over, the one named last changes fastest.
Arguments:
- hidden: bfloat16 [4, 1024, 4096], P('dp', 'ctx', 'tp'), may hold values from -6 to 6
- target: bfloat16 [4, 1024, 4096], P('dp', 'ctx', 'tp'), may hold values from -24 to 24
- gain: float32 [4096], replicated, may hold values from 0.5 to 1.5
- w_query: bfloat16 [4096, 2048], P(('ctx', 'dp'), 'tp'), may hold values from -2.15625 to 2.15625
- w_key: bfloat16 [4096, 512], P(('ctx', 'dp'), 'tp'), may hold values from -0.09375 to 0.09375
- value_matrix: bfloat16 [4096, 512], P(('ctx', 'dp'), 'tp'), may hold values from -0.09375 to 0.09375
- w_out: bfloat16 [2048, 4096], P('tp', ('ctx', 'dp')), may hold values from -0.125 to 0.125
- block_order: int32 [4], replicated, may hold values from 0 to 3, each once
Outputs:
- branch: bfloat16 [4, 1024, 4096], P('dp', 'ctx', 'tp')
- loss: float32 [], replicated
Inputs may be any that keep to these rules, and one draw needn't show every extreme that they name: block_order is a permutation of 0 to 3.
All inputs are finite; a program needn't handle non-finite values.
Results may differ from a plain program's by a relative error of at most 0.013.
The roundings to bfloat16 on the way count: a program that leaves them out, or rounds other values in their place, can miss the bound.
Values may be sent and summed in bfloat16 or wider, within the bound.
A program may use at most 128 MiB of HBM per device.

v0:
```python
import jax
import jax.numpy as jnp
from jax import lax
from jax.sharding import PartitionSpec as P

MODEL_WIDTH = 4096
QUERY_HEADS = 16
KEY_VALUE_HEADS = 4
HEAD_SIZE = 128
rope_base = 500000.0


def shifted(value, axis, by):
    peers = lax.axis_size(axis)
    return lax.ppermute(value, axis, [(i, (i + by) % peers) for i in range(peers)])


def positions(order, start, rows, half):
    index = start + lax.iota(jnp.int32, rows)
    block = index // half
    slots = lax.iota(jnp.int32, order.shape[0])
    chosen = jnp.sum(jnp.where(block[:, None] == slots[None, :], order[None, :], 0), axis=1)
    return chosen * half + index % half


def apply_rotary(values, token_places):
    half = values.shape[-1] // 2
    freqs = rope_base ** (-(jnp.arange(half, dtype=jnp.float32) * 2.0) / values.shape[-1])
    angles = token_places.astype(jnp.float32)[:, None] * freqs[None, :]
    cosine = jnp.cos(angles)[:, None, :]
    sine = jnp.sin(angles)[:, None, :]
    first = values[..., :half]
    second = values[..., half:]
    return jnp.concatenate(
        [first * cosine - second * sine, second * cosine + first * sine], axis=-1
    )


def attend(state, query_rows, qpos, piece, kpos):
    peak, total, accum = state
    rows = piece.shape[1]
    local_heads = query_rows.shape[1]
    pair = piece.reshape(2, rows, local_heads, HEAD_SIZE)
    scores = jnp.einsum(
        "qcgd,kcd->cgqk", query_rows, pair[0], preferred_element_type=jnp.float32
    ) * (1.0 / HEAD_SIZE**0.5)
    allowed = (qpos[:, None] >= kpos[None, :])[None, None]
    scores = jnp.where(allowed, scores, -1e30)
    new_peak = jnp.maximum(peak, jnp.max(scores, axis=-1))
    weights = jnp.where(allowed, jnp.exp(scores - new_peak[..., None]), 0.0)
    factor = jnp.exp(peak - new_peak)
    total = total * factor + jnp.sum(weights, axis=-1)
    update = jnp.einsum(
        "cgqk,kcd->qcgd", weights.astype(jnp.bfloat16), pair[1], preferred_element_type=jnp.float32
    )
    accum = accum * jnp.transpose(factor, (2, 0, 1))[..., None] + update
    return (new_peak, total, accum)


def on_device(hidden, target, gain, w_query, w_key, value_matrix, w_out, block_order):
    rows = hidden.shape[1]
    half = rows // 2
    local = hidden[0]
    whole = lax.all_gather(local, "tp", axis=1, tiled=True)
    wide = whole.astype(jnp.float32)
    normed = (
        wide * lax.rsqrt(jnp.mean(wide * wide, axis=1, keepdims=True) + 1e-05) * gain[None, :]
    ).astype(jnp.bfloat16)
    pieces = (
        lax.all_gather(w_query, ("ctx", "dp"), axis=0, tiled=True),
        lax.all_gather(w_key, ("ctx", "dp"), axis=0, tiled=True),
        lax.all_gather(value_matrix, ("ctx", "dp"), axis=0, tiled=True),
    )
    query_rows, key, value_rows = tuple(
        (jnp.dot(normed, piece, preferred_element_type=jnp.float32) for piece in pieces)
    )
    shard = lax.axis_index("ctx")
    qpos = positions(block_order, shard * rows, rows, half)
    local_heads = w_key.shape[1] // HEAD_SIZE
    query_group = QUERY_HEADS // KEY_VALUE_HEADS
    query_rows = (
        apply_rotary(query_rows.reshape(rows, local_heads * query_group, HEAD_SIZE), qpos)
        .astype(jnp.bfloat16)
        .reshape(rows, local_heads, query_group, HEAD_SIZE)
    )
    key = (
        apply_rotary(key.reshape(rows, local_heads, HEAD_SIZE), qpos)
        .astype(jnp.bfloat16)
        .reshape(rows, local_heads * HEAD_SIZE)
    )
    pair = jnp.stack([key, value_rows.astype(jnp.bfloat16)])
    state = (
        jnp.full((local_heads, query_group, rows), -1e30, jnp.float32),
        jnp.zeros((local_heads, query_group, rows), jnp.float32),
        jnp.zeros((rows, local_heads, query_group, HEAD_SIZE), jnp.float32),
    )
    count = lax.axis_size("ctx")
    state = attend(state, query_rows, qpos, pair, qpos)

    def turn(step, carry):
        moved, inner = carry
        moved = shifted(moved, "ctx", 1)
        source = (shard - step) % count
        return (
            moved,
            attend(
                inner, query_rows, qpos, moved, positions(block_order, source * rows, rows, half)
            ),
        )

    moved_end, state = lax.fori_loop(1, count, turn, (pair, state))
    peak, total, accum = state
    attn = (
        (accum / jnp.transpose(total, (2, 0, 1))[..., None])
        .astype(jnp.bfloat16)
        .reshape(rows, local_heads * query_group * HEAD_SIZE)
    )
    terms = jnp.dot(
        attn,
        lax.all_gather(w_out, ("ctx", "dp"), axis=1, tiled=True),
        preferred_element_type=jnp.float32,
    )
    summed = lax.psum_scatter(terms.astype(jnp.bfloat16), "tp", scatter_dimension=1, tiled=True)
    resid = local.astype(jnp.float32) + summed.astype(jnp.float32) - target[0].astype(jnp.float32)
    squares = lax.psum(jnp.sum(resid * resid), ("ctx", "tp", "dp"))
    loss = squares / (lax.axis_size("dp") * lax.axis_size("ctx") * rows * MODEL_WIDTH)
    return (summed[None], loss)


def solution(mesh):
    in_specs = (
        P("dp", "ctx", "tp"),
        P("dp", "ctx", "tp"),
        P(),
        P(("ctx", "dp"), "tp"),
        P(("ctx", "dp"), "tp"),
        P(("ctx", "dp"), "tp"),
        P("tp", ("ctx", "dp")),
        P(),
    )
    out_specs = (P("dp", "ctx", "tp"), P())
    return jax.shard_map(
        on_device, mesh=mesh, in_specs=in_specs, out_specs=out_specs, check_vma=False
    )
```

profile of v0, /device:TPU:0, one launch (start us, length us, event | category | flops | bytes accessed | tf_op | source)
XLA Modules:
  0.0 378.8 jit_solution(6131819200116777629)
XLA Ops:
  7.2 0.0 copy-start.4
  7.2 0.0 all-gather.15.cloned.1.call-start
  7.2 0.7 all-gather.15.cloned.1.call-update
  7.9 0.0 all-gather.7.cloned.1.call-start
  8.0 0.7 all-gather.7.cloned.1.call-update
  8.7 0.0 all-gather.11.cloned.1.call-start
  8.7 0.7 all-gather.11.cloned.1.call-update
  9.4 0.0 all-gather.9.cloned.1.call-start
  9.4 0.5 all-gather.9.cloned.1.call-update
  10.0 0.0 all-gather.13.cloned.1.call-start
  10.0 0.5 all-gather.13.cloned.1.call-update
  10.6 0.0 reduce-scatter.2.cloned.1.call-start
  10.7 0.7 select_reduce_fusion
  11.4 1.8 multiply_cosine_fusion
  13.2 0.4 broadcast_compare_fusion
  13.6 33.2 %all-gather.15.cloned.1.call-done = bf16[1,512,4096]{2,1,0:T(8,128)(2,1)} async-done(((bf16[1,512,1024]{2,1,0:T(8,128)(2,1)}), bf16[1,512,4096]{2,1,0:T(8,128)(2,1)}) %all-gather.15.cloned.1.call-update) | async-done | bytes 4194320 | tf_op jit(solution)/shard_map/all_gather | solution.py:64
  46.8 3.1 fusion
  49.9 39.3 %all-gather.7.cloned.1.call-done = bf16[4096,128]{1,0:T(8,128)(2,1)} async-done(((bf16[512,128]{1,0:T(8,128)(2,1)}), bf16[4096,128]{1,0:T(8,128)(2,1)}) %all-gather.7.cloned.1.call-update) | async-done | bytes 1048592 | tf_op jit(solution)/shard_map/all_gather | solution.py:71
  89.2 0.0 copy-done.4
  89.2 4.1 %convolution_bitcast_fusion = f32[512,1,128]{0,2,1:T(8,128)S(1)} fusion(bf16[4096,128]{1,0:T(8,128)(2,1)} %all-gather.7.cloned.1.call-done, bf16[1,512,4096]{2,1,0:T(8,128)(2,1)} %all-gather.15.cloned.1.call-done, f32[4096]{0:T(1024)S(1)} %copy-done.4, f32[512]{0:T(512)S(1)} %add_rsqrt_fusion), kind=kOutput, calls=%fused_computation.31 | convolution fusion | flops 545259520 | bytes 5523456 | tf_op jit(solution)/shard_map/dot_general | solution.py:75
  93.3 0.6 fusion.41
  93.9 36.5 %all-gather.11.cloned.1.call-done = bf16[4096,128]{1,0:T(8,128)(2,1)} async-done(((bf16[512,128]{1,0:T(8,128)(2,1)}), bf16[4096,128]{1,0:T(8,128)(2,1)}) %all-gather.11.cloned.1.call-update) | async-done | bytes 1048592 | tf_op jit(solution)/shard_map/all_gather | solution.py:72
  130.4 4.1 %convolution_convert_fusion.1 = bf16[512,128]{0,1:T(8,128)(2,1)S(1)} fusion(bf16[4096,128]{1,0:T(8,128)(2,1)} %all-gather.11.cloned.1.call-done, bf16[1,512,4096]{2,1,0:T(8,128)(2,1)} %all-gather.15.cloned.1.call-done, f32[4096]{0:T(1024)S(1)} %copy-done.4, f32[512]{0:T(512)S(1)} %add_rsqrt_fusion), kind=kOutput, calls=%fused_computation.32 | convolution fusion | flops 545325056 | bytes 5392384 | tf_op jit(solution)/shard_map/dot_general | solution.py:75
  134.5 0.0 copy-start.2
  134.5 0.8 pad_maximum_fusion.1
  135.3 0.6 collective-permute-start
  135.9 0.0 copy-done.2
  135.9 68.1 %all-gather.9.cloned.1.call-done = bf16[4096,512]{1,0:T(8,128)(2,1)} async-done(((bf16[512,512]{1,0:T(8,128)(2,1)}), bf16[4096,512]{1,0:T(8,128)(2,1)}) %all-gather.9.cloned.1.call-update) | async-done | bytes 4194320 | tf_op jit(solution)/shard_map/all_gather | solution.py:70
  203.9 5.9 %fusion.74 = f32[512,512]{0,1:T(8,128)S(1)} fusion(bf16[4096,512]{1,0:T(8,128)(2,1)} %all-gather.9.cloned.1.call-done, bf16[1,512,4096]{2,1,0:T(8,128)(2,1)} %all-gather.15.cloned.1.call-done, f32[4096]{0:T(1024)S(1)} %copy-done.4, f32[512]{0:T(512)S(1)} %add_rsqrt_fusion), kind=kOutput, calls=%fused_computation.109 | convolution fusion | flops 2155872256 | bytes 9455616 | tf_op jit(solution)/shard_map/dot_general | solution.py:75
  209.9 0.1 fusion.79
  210.0 0.3 copy.31
  210.3 0.3 copy.32
  210.6 1.2 subtract_convert_fusion
  211.9 1.2 fusion.3
  213.1 0.0 collective-permute-done
  213.1 2.1 fusion.4
  215.2 0.0 copy-start.3
  215.3 1.0 fusion.5
  216.3 1.2 fusion.7
  217.6 0.0 copy-done.3
  217.6 1.3 fusion.28
  218.9 2.2 divide_convert_fusion
  221.1 57.8 %all-gather.13.cloned.1.call-done = bf16[512,4096]{1,0:T(8,128)(2,1)} async-done(((bf16[512,512]{1,0:T(8,128)(2,1)}), bf16[512,4096]{1,0:T(8,128)(2,1)}) %all-gather.13.cloned.1.call-update) | async-done | bytes 4194320 | tf_op jit(solution)/shard_map/all_gather | solution.py:120
  279.0 6.5 %convolution_convert_fusion = bf16[512,4096]{1,0:T(8,128)(2,1)} fusion(bf16[512,512]{0,1:T(8,128)(2,1)S(1)} %bitcast.172, bf16[512,4096]{1,0:T(8,128)(2,1)} %all-gather.13.cloned.1.call-done), kind=kOutput, calls=%fused_computation.5 | convolution fusion | flops 2149580800 | bytes 8912896 | tf_op jit(solution)/shard_map/dot_general | solution.py:118
  285.5 0.0 copy-start
  285.5 0.0 copy-start.1
  285.5 0.0 reduce-scatter.2.cloned.1.call-update
  285.6 42.7 %reduce-scatter.2.cloned.1.call-done = bf16[512,1024]{1,0:T(8,128)(2,1)} async-done(((bf16[512,4096]{1,0:T(8,128)(2,1)}), bf16[512,1024]{1,0:T(8,128)(2,1)}) %reduce-scatter.2.cloned.1.call-update) | async-done | bytes 1048592 | tf_op jit(solution)/shard_map/reduce_scatter | solution.py:123
  328.3 0.0 copy-done
  328.3 0.0 copy-done.1
  328.3 2.4 fusion.12
  330.7 39.5 %psum.7 = f32[]{:T(128)} all-reduce(f32[]{:T(128)} %fusion.12), channel_id=1, replica_groups=mesh['ctx'=2,'tp'=4,'dp'=4] {'ctx','tp','dp'}, use_global_device_ids=true, to_apply=%region_9.10 | all-reduce | flops 1 | bytes 8 | tf_op jit(solution)/shard_map/psum | solution.py:125
  (7 shorter events, 0.1 us)
Async XLA Ops:
  7.2 82.0 %copy-start.4 = (f32[4096]{0:T(1024)S(1)}, f32[4096]{0:T(1024)}, u32[]{:S(2)}) copy-start(f32[4096]{0:T(1024)} %param.10) | copy-start | bytes 49156
  7.2 39.6 %all-gather.15.cloned.1.call-start = ((), (), s32[]{:S(2)}) async-start(), calls=%async_computation.6 | async-start | bytes 5242880 | tf_op jit(solution)/shard_map/all_gather | solution.py:64
  7.9 81.3 %all-gather.7.cloned.1.call-start = ((), (), s32[]{:S(2)}) async-start(), calls=%async_computation.1 | async-start | bytes 1179648 | tf_op jit(solution)/shard_map/all_gather | solution.py:71
  8.7 121.8 %all-gather.11.cloned.1.call-start = ((), (), s32[]{:S(2)}) async-start(), calls=%async_computation.3 | async-start | bytes 1179648 | tf_op jit(solution)/shard_map/all_gather | solution.py:72
  9.4 194.5 %all-gather.9.cloned.1.call-start = ((), (), s32[]{:S(2)}) async-start(), calls=%async_computation.2 | async-start | bytes 4718592 | tf_op jit(solution)/shard_map/all_gather | solution.py:70
  10.0 269.0 %all-gather.13.cloned.1.call-start = ((), (), s32[]{:S(2)}) async-start(), calls=%async_computation.4 | async-start | bytes 4718592 | tf_op jit(solution)/shard_map/all_gather | solution.py:120
  10.6 317.7 %reduce-scatter.2.cloned.1.call-start = ((), (), s32[]{:S(2)}) async-start(), calls=%async_computation.5 | async-start | bytes 5242880 | tf_op jit(solution)/shard_map/reduce_scatter | solution.py:123
  134.5 1.4 copy-start.2
  135.3 77.8 %collective-permute-start = (bf16[2,512,128]{1,2,0:T(8,128)(2,1)}, bf16[2,512,128]{1,2,0:T(8,128)(2,1)}, u32[]{:S(2)}, u32[]{:S(2)}) collective-permute-start(bf16[2,512,128]{1,2,0:T(8,128)(2,1)} %pad_maximum_fusion.1), channel_id=1, source_target_pairs={{0,16},{16,0},{1,17},{17,1},{2,18},{18,2},{3,19},{19,3},{4,20},{20... | collective-permute-start | bytes 786440 | tf_op jit(solution)/shard_map/while/body/eval_jaxpr/ppermute | solution.py:15
  215.2 2.3 copy-start.3
  285.5 42.8 %copy-start = (bf16[1,512,1024]{2,1,0:T(8,128)(2,1)S(1)}, bf16[1,512,1024]{2,1,0:T(8,128)(2,1)}, u32[]{:S(2)}) copy-start(bf16[1,512,1024]{2,1,0:T(8,128)(2,1)} %param.8) | copy-start | bytes 3145732
  285.5 42.8 %copy-start.1 = (bf16[1,512,1024]{2,1,0:T(8,128)(2,1)S(1)}, bf16[1,512,1024]{2,1,0:T(8,128)(2,1)}, u32[]{:S(2)}) copy-start(bf16[1,512,1024]{2,1,0:T(8,128)(2,1)} %param.9) | copy-start | bytes 3145732
Sparse Core Ops, SparseCore 0:
  9.5 37.1 all-gather.14
  48.9 40.2 all-gather.6
  91.3 39.0 all-gather.10
  132.4 71.5 all-gather.8
  205.8 73.1 all-gather.12
  285.7 42.5 reduce-scatter.1
where the time goes:
time: 379 us
  waiting for transfers between devices  281 us (74%)
  blocking collectives  39.5 us (10%)
  matrix products  27.6 us (7%)
  between operations  16.1 us (4%)
  other arithmetic  13.3 us (4%)
    all_gather x1, waiting for transfers between devices, on_device(): lax.all_gather(w_query, ('ctx', 'dp'), axis=0, tiled=True)  68.1 us
    all_gather x1, waiting for transfers between devices, on_device(): lax.all_gather(w_out, ('ctx', 'dp'), axis=1, tiled=True)  57.8 us
    reduce_scatter x1, waiting for transfers between devices, on_device(): lax.psum_scatter(terms.astype(jnp.bfloat16), 'tp', scatter_dimension=1, t...  42.7 us
    psum x1, blocking collectives, on_device(): squares = lax.psum(jnp.sum(resid * resid), ('ctx', 'tp', 'dp'))  39.5 us
    all_gather x1, waiting for transfers between devices, on_device(): lax.all_gather(w_key, ('ctx', 'dp'), axis=0, tiled=True)  39.3 us
    all_gather x1, waiting for transfers between devices, on_device(): lax.all_gather(value_matrix, ('ctx', 'dp'), axis=0, tiled=True)  36.5 us
    all_gather x1, waiting for transfers between devices, on_device(): whole = lax.all_gather(local, 'tp', axis=1, tiled=True)  33.2 us
    dot_general x3, matrix products, on_device(): jnp.dot(normed, piece, preferred_element_type=jnp.float32)  14.1 us
  transfers between devices with their start and end apart: 7, of which 6 were waited for; matrix products, arithmetic and copies ran while one was open for 9% of the time, Pallas kernels for 0%

commit v1 on v0

--- a/solution.py
+++ b/solution.py
@@ -61,7 +61,12 @@
     rows = hidden.shape[1]
     half = rows // 2
     local = hidden[0]
-    whole = lax.all_gather(local, "tp", axis=1, tiled=True)
+    ring = [local]
+    for hop in range(3):
+        ring.append(lax.ppermute(ring[-1], "tp", [(dev, (dev + 1) % 4) for dev in range(4)]))
+    whole = jnp.roll(
+        jnp.concatenate(ring[::-1], axis=1), (lax.axis_index("tp") + 1) * ring[0].shape[1], axis=1
+    )
     wide = whole.astype(jnp.float32)
     normed = (
         wide * lax.rsqrt(jnp.mean(wide * wide, axis=1, keepdims=True) + 1e-05) * gain[None, :]

time: 379 us -> 343 us (0.905)
  waiting for transfers between devices: 281 us -> 236 us
  local copies, waits for them, and re-layouts: 0.75 us -> 9.67 us
    ppermute x0 -> x3, waiting for transfers between devices: none -> 39.4 us  [on_device(): lax.ppermute(ring[-1], 'tp', [(dev, (dev + 1) % 4) for dev in range(4)])]
    all_gather x1, waiting for transfers between devices: 39.3 us -> 0.02 us  [on_device(): lax.all_gather(w_key, ('ctx', 'dp'), axis=0, tiled=True)]
    all_gather x1 -> x0, waiting for transfers between devices: 33.2 us -> none  [on_device(): whole = lax.all_gather(local, 'tp', axis=1, tiled=True)]
    unnamed x12 -> x23, local copies, waits for them, and re-layouts: 0.68 us -> 8.7 us
    all_gather x1, waiting for transfers between devices: 36.5 us -> 28.9 us  [on_device(): lax.all_gather(value_matrix, ('ctx', 'dp'), axis=0, tiled=True)]
  transfers between devices with their start and end apart: 7 -> 9, of which waited for: 6 -> 7; matrix products, arithmetic and copies ran while one was open for 9% -> 11% of each run, Pallas kernels for 0% -> 0%
where the time goes in v1:
time: 343 us; the launch traced here: 342 us
  waiting for transfers between devices  236 us (69%)
  blocking collectives  39.5 us (12%)
  matrix products  28.6 us (8%)
  between operations  15.9 us (5%)
  other arithmetic  11.8 us (3%)
  local copies, waits for them, and re-layouts  9.67 us (3%)
    all_gather x1, waiting for transfers between devices, on_device(): lax.all_gather(w_query, ('ctx', 'dp'), axis=0, tiled=True)  67.6 us
    all_gather x1, waiting for transfers between devices, on_device(): lax.all_gather(w_out, ('ctx', 'dp'), axis=1, tiled=True)  54.9 us
    reduce_scatter x1, waiting for transfers between devices, on_device(): lax.psum_scatter(terms.astype(jnp.bfloat16), 'tp', scatter_dimension=1, t...  42.7 us
    psum x1, blocking collectives, on_device(): squares = lax.psum(jnp.sum(resid * resid), ('ctx', 'tp', 'dp'))  39.5 us
    ppermute x3, waiting for transfers between devices, on_device(): lax.ppermute(ring[-1], 'tp', [(dev, (dev + 1) % 4) for dev in range(4)])  39.4 us
    all_gather x1, waiting for transfers between devices, on_device(): lax.all_gather(value_matrix, ('ctx', 'dp'), axis=0, tiled=True)  28.9 us
    dot_general x3, matrix products, on_device(): jnp.dot(normed, piece, preferred_element_type=jnp.float32)  14.2 us
    unnamed x23, local copies, waits for them, and re-layouts  8.7 us
  transfers between devices with their start and end apart: 9, of which 7 were waited for; matrix products, arithmetic and copies ran while one was open for 11% of the time, Pallas kernels for 0%

profile of v1, /device:TPU:0, one launch (start us, length us, event | category | flops | bytes accessed | tf_op | source)
XLA Modules:
  0.0 342.5 jit_solution(18265280814586790945)
XLA Ops:
  7.2 0.0 all-gather.5.cloned.1.call-start
  7.2 0.7 all-gather.5.cloned.1.call-update
  7.9 0.0 all-gather.9.cloned.1.call-start
  7.9 0.7 all-gather.9.cloned.1.call-update
  8.6 0.0 copy-start
  8.7 0.0 all-gather.7.cloned.1.call-start
  8.7 0.7 all-gather.7.cloned.1.call-update
  9.4 0.0 all-gather.11.cloned.1.call-start
  9.4 0.5 collective-permute-start
  10.0 14.6 %collective-permute-done = bf16[512,1024]{1,0:T(8,128)(2,1)S(1)} collective-permute-done((bf16[512,1024]{1,0:T(8,128)(2,1)}, bf16[512,1024]{1,0:T(8,128)(2,1)S(1)}, u32[]{:S(2)}, u32[]{:S(2)}) %collective-permute-start) | collective-permute-done | bytes 1048608 | tf_op jit(solution)/shard_map/ppermute | solution.py:66
  24.6 0.0 collective-permute-start.1
  24.7 0.0 all-gather.11.cloned.1.call-update
  24.7 0.0 reduce-scatter.2.cloned.1.call-start
  24.8 14.1 %collective-permute-done.1 = bf16[512,1024]{1,0:T(8,128)(2,1)S(1)} collective-permute-done((bf16[512,1024]{1,0:T(8,128)(2,1)S(1)}, bf16[512,1024]{1,0:T(8,128)(2,1)S(1)}, u32[]{:S(2)}, u32[]{:S(2)}) %collective-permute-start.1) | collective-permute-done | bytes 1048608 | tf_op jit(solution)/shard_map/ppermute | solution.py:66
  38.8 0.0 collective-permute-start.2
  38.9 0.7 select_reduce_fusion
  39.6 1.8 multiply_cosine_fusion
  41.5 1.0 broadcast_compare_fusion
  42.5 10.7 %collective-permute-done.2 = bf16[512,1024]{1,0:T(8,128)(2,1)} collective-permute-done((bf16[512,1024]{1,0:T(8,128)(2,1)S(1)}, bf16[512,1024]{1,0:T(8,128)(2,1)}, u32[]{:S(2)}, u32[]{:S(2)}) %collective-permute-start.2) | collective-permute-done | bytes 1048608 | tf_op jit(solution)/shard_map/ppermute | solution.py:66
  53.2 1.3 constant_dynamic-update-slice_fusion.7
  54.5 0.1 constant_dynamic-update-slice_fusion.6
  54.6 0.1 constant_dynamic-update-slice_fusion.5
  54.7 0.0 copy-done
  54.7 0.1 constant_dynamic-update-slice_fusion.4
  54.8 1.3 constant_dynamic-update-slice_fusion.3
  56.1 0.1 constant_dynamic-update-slice_fusion.2
  56.2 0.0 copy-start.6
  56.2 0.1 constant_dynamic-update-slice_fusion.1
  56.3 0.1 constant_dynamic-update-slice_fusion
  56.4 0.0 copy-start.1
  56.4 3.2 copy-done.1
  59.6 0.9 fusion
  60.5 0.0 all-gather.5.cloned.1.call-done
  60.6 0.0 copy-done.6
  60.6 4.2 %convolution_bitcast_fusion = f32[512,1,128]{0,2,1:T(8,128)S(1)} fusion(bf16[4096,128]{1,0:T(8,128)(2,1)} %all-gather.5.cloned.1.call-done, f32[4096]{0:T(1024)S(1)} %copy-done.6, f32[512]{0:T(512)S(1)} %add_rsqrt_fusion, bf16[512,8192]{1,0:T(8,128)(2,1)} %copy-done.1, s32[]{:T(128)S(6)} %select_n.92), kind=kOutput, calls=%fused_computation.30 | convolution fusion | flops 545259520 | bytes 5523460 | tf_op jit(solution)/shard_map/dot_general | solution.py:80
  64.8 0.6 fusion.41
  65.4 28.9 %all-gather.9.cloned.1.call-done = bf16[4096,128]{1,0:T(8,128)(2,1)} async-done(((bf16[512,128]{1,0:T(8,128)(2,1)}), bf16[4096,128]{1,0:T(8,128)(2,1)}) %all-gather.9.cloned.1.call-update) | async-done | bytes 1048592 | tf_op jit(solution)/shard_map/all_gather | solution.py:77
  94.3 4.1 %convolution_convert_fusion.1 = bf16[512,128]{0,1:T(8,128)(2,1)S(1)} fusion(bf16[4096,128]{1,0:T(8,128)(2,1)} %all-gather.9.cloned.1.call-done, f32[4096]{0:T(1024)S(1)} %copy-done.6, f32[512]{0:T(512)S(1)} %add_rsqrt_fusion, bf16[512,8192]{1,0:T(8,128)(2,1)} %copy-done.1, s32[]{:T(128)S(6)} %select_n.92), kind=kOutput, calls=%fused_computation.31 | convolution fusion | flops 545325056 | bytes 5392388 | tf_op jit(solution)/shard_map/dot_general | solution.py:80
  98.4 0.0 copy-start.4
  98.4 0.6 copy-done.4
  99.0 0.7 pad_maximum_fusion.1
  99.8 0.6 collective-permute-start.3
  100.4 67.6 %all-gather.7.cloned.1.call-done = bf16[4096,512]{1,0:T(8,128)(2,1)} async-done(((bf16[512,512]{1,0:T(8,128)(2,1)}), bf16[4096,512]{1,0:T(8,128)(2,1)}) %all-gather.7.cloned.1.call-update) | async-done | bytes 4194320 | tf_op jit(solution)/shard_map/all_gather | solution.py:75
  168.0 5.9 %fusion.74 = f32[512,512]{0,1:T(8,128)S(1)} fusion(bf16[4096,512]{1,0:T(8,128)(2,1)} %all-gather.7.cloned.1.call-done, f32[4096]{0:T(1024)S(1)} %copy-done.6, f32[512]{0:T(512)S(1)} %add_rsqrt_fusion, bf16[512,8192]{1,0:T(8,128)(2,1)} %copy-done.1, s32[]{:T(128)S(6)} %select_n.92), kind=kOutput, calls=%fused_computation.116 | convolution fusion | flops 2155872256 | bytes 9455620 | tf_op jit(solution)/shard_map/dot_general | solution.py:80
  173.9 0.9 fusion.79
  174.8 0.3 copy.31
  175.2 1.4 copy.32
  176.6 1.3 subtract_convert_fusion
  177.9 2.2 fusion.3
  180.1 0.0 copy-start.2
  180.1 0.0 collective-permute-done.3
  180.1 2.1 fusion.4
  182.2 0.0 copy-done.2
  182.3 0.0 copy-start.5
  182.3 1.1 fusion.5
  183.3 1.2 fusion.7
  184.6 1.3 fusion.28
  185.9 2.2 divide_convert_fusion
  188.2 54.9 %all-gather.11.cloned.1.call-done = bf16[512,4096]{1,0:T(8,128)(2,1)} async-done(((bf16[512,512]{1,0:T(8,128)(2,1)}), bf16[512,4096]{1,0:T(8,128)(2,1)}) %all-gather.11.cloned.1.call-update) | async-done | bytes 4194320 | tf_op jit(solution)/shard_map/all_gather | solution.py:125
  243.1 6.5 %convolution_convert_fusion = bf16[512,4096]{1,0:T(8,128)(2,1)} fusion(bf16[512,512]{0,1:T(8,128)(2,1)S(1)} %bitcast.167, bf16[512,4096]{1,0:T(8,128)(2,1)} %all-gather.11.cloned.1.call-done), kind=kOutput, calls=%fused_computation.5 | convolution fusion | flops 2149580800 | bytes 8912896 | tf_op jit(solution)/shard_map/dot_general | solution.py:123
  249.6 0.0 reduce-scatter.2.cloned.1.call-update
  249.6 42.7 %reduce-scatter.2.cloned.1.call-done = bf16[512,1024]{1,0:T(8,128)(2,1)} async-done(((bf16[512,4096]{1,0:T(8,128)(2,1)}), bf16[512,1024]{1,0:T(8,128)(2,1)}) %reduce-scatter.2.cloned.1.call-update) | async-done | bytes 1048592 | tf_op jit(solution)/shard_map/reduce_scatter | solution.py:128
  292.3 2.4 fusion.12
  294.7 39.5 %psum.7 = f32[]{:T(128)} all-reduce(f32[]{:T(128)} %fusion.12), channel_id=1, replica_groups=mesh['ctx'=2,'tp'=4,'dp'=4] {'ctx','tp','dp'}, use_global_device_ids=true, to_apply=%region_9.10 | all-reduce | flops 1 | bytes 8 | tf_op jit(solution)/shard_map/psum | solution.py:130
  (10 shorter events, 0.1 us)
Async XLA Ops:
  7.2 53.4 %all-gather.5.cloned.1.call-start = ((), (), s32[]{:S(2)}) async-start(), calls=%async_computation.1 | async-start | bytes 1179648 | tf_op jit(solution)/shard_map/all_gather | solution.py:76
  7.9 86.4 %all-gather.9.cloned.1.call-start = ((), (), s32[]{:S(2)}) async-start(), calls=%async_computation.3 | async-start | bytes 1179648 | tf_op jit(solution)/shard_map/all_gather | solution.py:77
  8.6 46.0 %copy-start = (bf16[1,512,1024]{2,1,0:T(8,128)(2,1)S(1)}, bf16[1,512,1024]{2,1,0:T(8,128)(2,1)}, u32[]{:S(2)}) copy-start(bf16[1,512,1024]{2,1,0:T(8,128)(2,1)} %param.8) | copy-start | bytes 3145732
  8.7 159.3 %all-gather.7.cloned.1.call-start = ((), (), s32[]{:S(2)}) async-start(), calls=%async_computation.2 | async-start | bytes 4718592 | tf_op jit(solution)/shard_map/all_gather | solution.py:75
  9.4 233.7 %all-gather.11.cloned.1.call-start = ((), (), s32[]{:S(2)}) async-start(), calls=%async_computation.4 | async-start | bytes 4718592 | tf_op jit(solution)/shard_map/all_gather | solution.py:125
  9.4 15.2 %collective-permute-start = (bf16[512,1024]{1,0:T(8,128)(2,1)}, bf16[512,1024]{1,0:T(8,128)(2,1)S(1)}, u32[]{:S(2)}, u32[]{:S(2)}) collective-permute-start(bf16[512,1024]{1,0:T(8,128)(2,1)} %bitcast.160), channel_id=1, source_target_pairs={{0,4},{4,8},{8,12},{12,0},{1,5},{5,9},{9,13},{13,1},{2,6},{6,10},{... | collective-permute-start | bytes 3145736 | tf_op jit(solution)/shard_map/ppermute | solution.py:66
  24.6 14.2 %collective-permute-start.1 = (bf16[512,1024]{1,0:T(8,128)(2,1)S(1)}, bf16[512,1024]{1,0:T(8,128)(2,1)S(1)}, u32[]{:S(2)}, u32[]{:S(2)}) collective-permute-start(bf16[512,1024]{1,0:T(8,128)(2,1)S(1)} %collective-permute-done), channel_id=1, source_target_pairs={{0,4},{4,8},{8,12},{12,0},{1,5},{5,9},{9,13},{13,1},{2,6},{6,10},{... | collective-permute-start | bytes 3145736 | tf_op jit(solution)/shard_map/ppermute | solution.py:66
  24.7 267.6 %reduce-scatter.2.cloned.1.call-start = ((), (), s32[]{:S(2)}) async-start(), calls=%async_computation.5 | async-start | bytes 5242880 | tf_op jit(solution)/shard_map/reduce_scatter | solution.py:128
  38.8 14.3 %collective-permute-start.2 = (bf16[512,1024]{1,0:T(8,128)(2,1)S(1)}, bf16[512,1024]{1,0:T(8,128)(2,1)}, u32[]{:S(2)}, u32[]{:S(2)}) collective-permute-start(bf16[512,1024]{1,0:T(8,128)(2,1)S(1)} %collective-permute-done.1), channel_id=1, source_target_pairs={{0,4},{4,8},{8,12},{12,0},{1,5},{5,9},{9,13},{13,1},{2,6},{6,10},{... | collective-permute-start | bytes 3145736 | tf_op jit(solution)/shard_map/ppermute | solution.py:66
  56.2 4.4 %copy-start.6 = (f32[4096]{0:T(1024)S(1)}, f32[4096]{0:T(1024)}, u32[]{:S(2)}) copy-start(f32[4096]{0:T(1024)} %param.10) | copy-start | bytes 49156
  56.4 3.2 copy-start.1
  98.4 0.7 copy-start.4
  99.8 80.3 %collective-permute-start.3 = (bf16[2,512,128]{1,2,0:T(8,128)(2,1)}, bf16[2,512,128]{1,2,0:T(8,128)(2,1)}, u32[]{:S(2)}, u32[]{:S(2)}) collective-permute-start(bf16[2,512,128]{1,2,0:T(8,128)(2,1)} %pad_maximum_fusion.1), channel_id=1, source_target_pairs={{0,16},{16,0},{1,17},{17,1},{2,18},{18,2},{3,19},{19,3},{4,20},{20... | collective-permute-start | bytes 786440 | tf_op jit(solution)/shard_map/while/body/eval_jaxpr/ppermute | solution.py:15
  180.1 2.2 copy-start.2
  182.3 2.3 copy-start.5
  249.6 42.8 %copy-start.3 = (bf16[1,512,1024]{2,1,0:T(8,128)(2,1)S(1)}, bf16[1,512,1024]{2,1,0:T(8,128)(2,1)}, u32[]{:S(2)}) copy-start(bf16[1,512,1024]{2,1,0:T(8,128)(2,1)} %param.9) | copy-start | bytes 3145732
Sparse Core Ops, SparseCore 0:
  10.1 42.9 all-gather.4
  55.3 38.9 all-gather.8
  96.4 71.5 all-gather.6
  169.9 73.1 all-gather.10
  249.7 42.5 reduce-scatter.1
